TPU v7x, 128 devices: a whole 4x4x4 slice. The times are simulated.
128 devices in a mesh: gx: 8 (over x, core), gy: 16 (over z, y).
Axes of the slice: x: 4, y: 4, z: 4, core: 2. Of those that a mesh axis runs over, the one named last changes fastest.
Arguments:
- mask_feats: bfloat16 [256, 8, 14, 14, 256], P(('gx', 'gy')), may hold values from -6 to 6
- mask_cot: bfloat16 [256, 8, 14, 14, 256], P(('gx', 'gy')), may hold values from -6 to 6
- roi_counts: int32 [256], P(('gx', 'gy')), may hold values from 1 to 8, as said below
- rpn_feats: bfloat16 [256, 48, 32, 256], P(('gx', 'gy')), may hold values from -6 to 6
- rpn_cot: bfloat16 [256, 48, 32, 256], P(('gx', 'gy')), may hold values from -360 to 360
- anchor_counts: int32 [256], P(('gx', 'gy')), may hold values from 32 to 223
- mask_weight: float32 [2304, 256], replicated, may hold values from -0.125 to 0.125
- rpn_weight: float32 [2304, 256], replicated, may hold values from -0.125 to 0.125
- mask_moment: float32 [2304, 256], replicated, may hold values from -6 to 6
- rpn_moment: float32 [2304, 256], replicated, may hold values from -6 to 6
Outputs:
- new_mask_weight: float32 [2304, 256], replicated
- new_rpn_weight: float32 [2304, 256], replicated
- new_mask_moment: float32 [2304, 256], replicated
- new_rpn_moment: float32 [2304, 256], replicated
Inputs may be any that keep to these rules, and one draw needn't show every extreme that they name: `roi_counts`: every image has at least one positive ROI; some image has all 8 slots positive.
All inputs are finite; a program needn't handle non-finite values.
Results may differ from a plain program's by a relative error of at most 0.0003.
Values sent between devices are 32-bit elements; how exact they have to be, the bound alone decides.
A program may use at most 128 MiB of HBM per device.

v0:
```python
import jax
import jax.numpy as jnp
from jax import lax
from jax.sharding import PartitionSpec as P


def weight_grad(feats, cotan):
    grid_rows = feats.shape[1]
    grid_cols = feats.shape[2]
    chans = feats.shape[3]
    padded = jnp.pad(feats, ((0, 0), (1, 1), (1, 1), (0, 0)))
    flat_cot = cotan.reshape(-1, chans)
    blocks = []
    for row_tap in range(3):
        for col_tap in range(3):
            window = padded[
                :, row_tap : row_tap + grid_rows, col_tap : col_tap + grid_cols, :
            ].reshape(-1, chans)
            blocks.append(
                lax.dot_general(
                    window, flat_cot, (((0,), (0,)), ((), ())), preferred_element_type=jnp.float32
                )
            )
    return jnp.concatenate(blocks, axis=0)


def step_update(weight, moment, grad):
    fresh_moment = 0.9 * moment + grad
    return (weight - 0.02 * fresh_moment, fresh_moment)


def on_device(
    mask_feats,
    mask_cot,
    roi_counts,
    rpn_feats,
    rpn_cot,
    anchor_counts,
    mask_weight,
    rpn_weight,
    mask_moment,
    rpn_moment,
):
    slot_count = mask_feats.shape[1]
    side = mask_feats.shape[2]
    chans = mask_feats.shape[4]
    slots = jnp.arange(slot_count, dtype=jnp.int32)
    valid_slots = (slots[None, :] < roi_counts[:, None]).astype(jnp.bfloat16)
    masked = mask_cot * valid_slots[:, :, None, None, None]
    mask_local = weight_grad(
        mask_feats.reshape(-1, side, side, chans), masked.reshape(-1, side, side, chans)
    )
    rpn_local = weight_grad(rpn_feats, rpn_cot)
    local_counts = jnp.stack([jnp.sum(roi_counts), jnp.sum(anchor_counts)]).astype(jnp.float32)
    mask_sum, rpn_sum, totals = lax.psum((mask_local, rpn_local, local_counts), ("gx", "gy"))
    mask_grad = mask_sum / totals[0]
    rpn_grad = rpn_sum / totals[1]
    new_mask_weight, new_mask_moment = step_update(mask_weight, mask_moment, mask_grad)
    new_rpn_weight, new_rpn_moment = step_update(rpn_weight, rpn_moment, rpn_grad)
    return (new_mask_weight, new_rpn_weight, new_mask_moment, new_rpn_moment)


def solution(mesh):
    placed = (
        P(("gx", "gy"), None, None, None, None),
        P(("gx", "gy"), None, None, None, None),
        P(("gx", "gy")),
        P(("gx", "gy"), None, None, None),
        P(("gx", "gy"), None, None, None),
        P(("gx", "gy")),
        P(),
        P(),
        P(),
        P(),
    )
    return jax.shard_map(
        on_device, mesh=mesh, in_specs=placed, out_specs=(P(), P(), P(), P()), check_vma=False
    )
```

profile of v0, /device:TPU:1, one launch (start us, length us, event | category | flops | bytes accessed | tf_op | source)
XLA Modules:
  0.0 269.6 jit_solution(1782575717403272848)
XLA Ops:
  8.1 1.6 broadcast_multiply_fusion
  9.7 1.6 copy.29
  11.3 3.7 %reshape_reshape.3 = bf16[3136,256]{1,0:T(8,128)(2,1)} reshape(bf16[2,8,14,14,256]{4,3,2,1,0:T(8,128)(2,1)} %copy.29) | data formatting | bytes 3211264 | tf_op jit(solution)/shard_map/reshape;reshape | solution.py:12
  15.0 1.6 copy.81
  16.5 4.3 %pad_slice_fusion = (bf16[16,14,14,256]{3,0,2,1:T(8,128)(2,1)}, bf16[16,14,14,256]{3,0,2,1:T(8,128)(2,1)}, bf16[16,14,14,256]{3,0,2,1:T(8,128)(2,1)}, bf16[16,14...) fusion(bf16[16,14,14,256]{3,0,2,1:T(8,128)(2,1)S(1)} %bitcast.89), kind=kLoop, calls=%fused_computation.4 | loop fusion | bytes 14450688 | tf_op jit(solution)/shard_map/slice | solution.py:16
  20.8 1.8 copy.28
  22.7 3.6 %reshape.70 = bf16[3136,256]{1,0:T(8,128)(2,1)} reshape(bf16[16,14,14,256]{3,2,1,0:T(8,128)(2,1)} %copy.28) | data formatting | bytes 3211264 | tf_op jit(solution)/shard_map/reshape | solution.py:18
  26.3 3.3 %copy.30 = bf16[16,14,14,256]{3,2,1,0:T(8,128)(2,1)} copy(bf16[16,14,14,256]{3,0,2,1:T(8,128)(2,1)} %get-tuple-element.11) | data formatting | bytes 3211264 | tf_op jit(solution)/shard_map/slice | solution.py:16
  29.6 3.6 %reshape.71 = bf16[3136,256]{1,0:T(8,128)(2,1)} reshape(bf16[16,14,14,256]{3,2,1,0:T(8,128)(2,1)} %copy.30) | data formatting | bytes 3211264 | tf_op jit(solution)/shard_map/reshape | solution.py:18
  33.2 3.3 %copy.31 = bf16[16,14,14,256]{3,2,1,0:T(8,128)(2,1)} copy(bf16[16,14,14,256]{3,0,2,1:T(8,128)(2,1)} %get-tuple-element.12) | data formatting | bytes 3211264 | tf_op jit(solution)/shard_map/slice | solution.py:16
  36.5 3.6 %reshape.72 = bf16[3136,256]{1,0:T(8,128)(2,1)} reshape(bf16[16,14,14,256]{3,2,1,0:T(8,128)(2,1)} %copy.31) | data formatting | bytes 3211264 | tf_op jit(solution)/shard_map/reshape | solution.py:18
  40.1 3.3 %copy.32 = bf16[16,14,14,256]{3,2,1,0:T(8,128)(2,1)} copy(bf16[16,14,14,256]{3,0,2,1:T(8,128)(2,1)} %get-tuple-element.13) | data formatting | bytes 3211264 | tf_op jit(solution)/shard_map/slice | solution.py:16
  43.3 3.6 %reshape.73 = bf16[3136,256]{1,0:T(8,128)(2,1)} reshape(bf16[16,14,14,256]{3,2,1,0:T(8,128)(2,1)} %copy.32) | data formatting | bytes 3211264 | tf_op jit(solution)/shard_map/reshape | solution.py:18
  47.0 3.4 %convolution_dynamic-update-slice_fusion.7 = f32[2304,256]{1,0:T(8,128)} fusion(bf16[3136,256]{1,0:T(8,128)(2,1)} %reshape.70, bf16[3136,256]{1,0:T(8,128)(2,1)} %reshape_reshape.3), kind=kOutput, calls=%fused_computation.36 | convolution fusion | flops 411041792 | bytes 3473408 | tf_op jit(solution)/shard_map/dot_general | solution.py:20
  54.7 1.5 fusion.25
  56.8 1.4 reshape.74
  58.2 2.0 copy.36
  60.2 1.4 reshape.75
  61.6 2.0 copy.37
  63.6 1.4 reshape.76
  65.0 2.0 copy.38
  67.1 1.4 reshape.77
  68.5 2.3 copy.39
  70.8 1.8 fusion.24
  72.6 2.1 fusion.22
  74.7 2.0 fusion.20
  80.1 2.1 fusion.14
  82.2 2.3 fusion.12
  84.5 2.1 fusion.10
  96.5 69.6 %psum.22 = f32[2]{0:T(128)S(1)} all-reduce(f32[2]{0:T(128)S(1)} %add_convert_fusion), channel_id=1, replica_groups=mesh['gx'=8,'gy'=16] {'gx','gy'}, use_global_device_ids=true, to_apply=%region_3.4 | all-reduce | flops 2 | bytes 16 | tf_op jit(solution)/shard_map/psum | solution.py:55
  166.7 85.5 %all-reduce.5.cloned.1.call-done = (f32[2304,256]{1,0:T(8,128)}, f32[2304,256]{1,0:T(8,128)}) async-done(((f32[2304,256]{1,0:T(8,128)}, f32[2304,256]{1,0:T(8,128)}), (f32[2304,256]{1,0:T(8,128)}, f32[2304,256]{1,0:T(8,128)})) %all-reduce.5.cloned.1.call-update) | async-done | bytes 4718608 | tf_op jit(solution)/shard_map/psum | solution.py:55
  252.2 10.6 %multiply_subtract_fusion = (f32[2304,256]{1,0:T(8,128)}, f32[2304,256]{1,0:T(8,128)}, f32[2304,256]{1,0:T(8,128)}, f32[2304,256]{1,0:T(8,128)}) fusion(f32[2304,256]{1,0:T(8,128)} %param.17, f32[2304,256]{1,0:T(8,128)} %get-tuple-element.5, f32[]{:T(128)} %bitcast.25, f32[2304,256]{1,0:T(8,128)} %param.19, f32[2304,256]{1,0:T(8,128)} %param.16, ...), kind=kLoop, calls=%fused_computation | loop fusion | flops 5898240 | bytes 23592968 | tf_op jit(solution)/shard_map/sub | solution.py:29
  (50 shorter events, 19.6 us)
Async XLA Ops:
  7.2 63.6 %copy-start = (bf16[2,48,32,256]{3,2,1,0:T(8,128)(2,1)S(1)}, bf16[2,48,32,256]{3,2,1,0:T(8,128)(2,1)}, u32[]{:S(2)}) copy-start(bf16[2,48,32,256]{3,2,1,0:T(8,128)(2,1)} %param.14) | copy-start | bytes 4718596
  7.2 245.1 %all-reduce.5.cloned.1.call-start = ((), (), s32[]{:S(2)}) async-start(), calls=%async_computation | async-start | bytes 9437184 | tf_op jit(solution)/shard_map/psum | solution.py:55
  47.0 3.4 %copy-start.5 = (bf16[3136,256]{1,0:T(8,128)(2,1)S(1)}, bf16[3136,256]{1,0:T(8,128)(2,1)}, u32[]{:S(2)}) copy-start(bf16[3136,256]{1,0:T(8,128)(2,1)} %reshape_reshape.3) | copy-start | bytes 4816900
  47.0 3.4 %copy-start.11 = (bf16[3136,256]{1,0:T(8,128)(2,1)S(1)}, bf16[3136,256]{1,0:T(8,128)(2,1)}, u32[]{:S(2)}) copy-start(bf16[3136,256]{1,0:T(8,128)(2,1)} %reshape.71) | copy-start | bytes 4816900
  50.4 1.4 copy-start.12
  51.8 1.4 copy-start.13
  53.2 1.4 copy-start.2
  54.6 1.5 copy-start.1
  76.7 1.4 copy-start.3
  84.5 2.1 copy-start.6
  84.5 2.1 copy-start.7
  86.6 1.5 copy-start.4
  86.6 2.4 copy-start.8
  89.0 1.4 copy-start.9
  90.4 1.4 copy-start.10
  93.2 0.7 copy-start.14
  93.2 1.3 copy-start.15
Sparse Core Ops, SparseCore 0:
  93.3 158.8 all-reduce.4
where the time goes:
time: 271 us; the launch traced here: 270 us
  waiting for transfers between devices  85.5 us (32%)
  blocking collectives  69.6 us (26%)
  local copies, waits for them, and re-layouts  54.6 us (20%)
  matrix products  30 us (11%)
  other arithmetic  15.6 us (6%)
  between operations  14.2 us (5%)
    psum x1, waiting for transfers between devices, on_device(): lax.psum((mask_local, rpn_local, local_counts), ('gx', 'gy'))  85.5 us
    psum x1, blocking collectives, on_device(): lax.psum((mask_local, rpn_local, local_counts), ('gx', 'gy'))  69.6 us
    dot_general x18, matrix products, weight_grad(): lax.dot_general(window, flat_cot, (((0,), (0,)), ((), ())), preferred_ele...  30 us
    slice x9, local copies, waits for them, and re-layouts, weight_grad(): padded[:, row_tap:row_tap + grid_rows, col_tap:col_tap + grid_cols, :]  22.6 us
    reshape x8, local copies, waits for them, and re-layouts, weight_grad(): window = padded[:, row_tap:row_tap + grid_rows, col_tap:col_tap + grid_co...  20.2 us
    sub x1, other arithmetic, step_update(): return (weight - 0.02 * fresh_moment, fresh_moment)  10.6 us
    unnamed x34, local copies, waits for them, and re-layouts  5.92 us
  transfers between devices with their start and end apart: 1, of which 1 were waited for; matrix products, arithmetic and copies ran while one was open for 1% of the time, Pallas kernels for 0%

commit v1 on v0

v1 whole, which is shorter than its diff:
```python
import jax
import jax.numpy as jnp
from jax import lax
from jax.experimental import pallas as pl
from jax.experimental.pallas import tpu as pltpu
from jax.sharding import PartitionSpec as P

bf16 = jnp.bfloat16
f32 = jnp.float32
RING = 4
PLANE = sorted(
    ((db, dc) for db in range(4) for dc in range(4) if (db, dc) != (0, 0)),
    key=lambda d: min(d[0], 4 - d[0]) + min(d[1], 4 - d[1]),
)
CUBE = [
    (dx, dy, dz)
    for dx in range(4)
    for dy in range(4)
    for dz in range(4)
    if 1 <= (dx != 0) + (dy != 0) + (dz != 0) <= 2
]


def kernel(
    xm_hbm, ym_hbm, roi, xr_hbm, yr_hbm, anchor, wm_hbm, wr_hbm, mm_hbm, mr_hbm,
    out_wm, out_wr, out_mm, out_mr,
    xm, ym, xr, yr, xt, grad, other, part, inbox, relay, chunk, plane_in, full,
    weights, moments, count, count_in,
    load_sem, pair_send, pair_recv, ring_send, ring_recv, plane_send, plane_recv,
    fan_send, fan_recv, ag_send, ag_recv, last_send, last_recv, count_send, count_recv,
):
    gx = lax.axis_index("gx")
    gy = lax.axis_index("gy")
    core = lax.rem(gx, 2)
    pos = (gx // 2, lax.rem(gy, 4), gy // 4)

    def at(offset, own_core=True):
        x, y, z = (lax.rem(p + d, RING) if d else p for p, d in zip(pos, offset))
        return (x * 2 + (core if own_core else 1 - core), z * 4 + y)

    def along(axis, d):
        offset = [0, 0, 0]
        offset[axis] = d % RING
        return at(offset)

    def send(src, dst, send_sem, recv_sem, device):
        copy = pltpu.make_async_remote_copy(
            src_ref=src, dst_ref=dst, send_sem=send_sem, recv_sem=recv_sem,
            device_id=device, device_id_type=pl.DeviceIdType.MESH,
        )
        copy.start()
        sent.append(copy)
        return copy

    sent = []
    partner = at((0, 0, 0), own_core=False)

    barrier = pltpu.get_barrier_semaphore()
    for device in [partner] + [at(o) for o in CUBE]:
        pl.semaphore_signal(barrier, inc=1, device_id=device, device_id_type=pl.DeviceIdType.MESH)

    loads = [
        pltpu.make_async_copy(xm_hbm, xm.at[:, :, pl.ds(1, 14)], load_sem.at[0]),
        pltpu.make_async_copy(ym_hbm, ym.at[:, pl.ds(1, 14)], load_sem.at[1]),
        pltpu.make_async_copy(xr_hbm, xr, load_sem.at[2]),
        pltpu.make_async_copy(yr_hbm.at[pl.ds(0, 1536)], yr.at[pl.ds(32, 1536)], load_sem.at[3]),
        pltpu.make_async_copy(yr_hbm.at[pl.ds(1536, 1536)], yr.at[pl.ds(1632, 1536)], load_sem.at[4]),
        pltpu.make_async_copy(mm_hbm, moments.at[0], load_sem.at[5]),
        pltpu.make_async_copy(mr_hbm, moments.at[1], load_sem.at[6]),
        pltpu.make_async_copy(wm_hbm, weights.at[0], load_sem.at[7]),
        pltpu.make_async_copy(wr_hbm, weights.at[1], load_sem.at[8]),
    ]
    for copy in loads[:5]:
        copy.start()
    for i in range(2):
        for e in (0, 15):
            xm[i, :, e] = jnp.zeros((14, 8, 256), bf16)
            ym[i, e] = jnp.zeros((14, 8, 256), bf16)
        for e in (0, 49):
            yr[pl.ds(1600 * i + 32 * e, 32), :] = jnp.zeros((32, 256), bf16)

    count[0, 0] = jnp.full((8, 128), (roi[0] + roi[1]).astype(f32))
    count[0, 1] = jnp.full((8, 128), (anchor[0] + anchor[1]).astype(f32))

    def prepare_mask():
        slot = lax.broadcasted_iota(jnp.int32, (8, 256), 0)

        def tap(b, carry):
            for i in range(2):
                keep = slot < roi[i]
                v = xm[i, :, pl.ds(b, 14)]
                v = jnp.where(keep[None, None], v, jnp.zeros_like(v))
                xt[pl.ds(pl.multiple_of(b * 256, 256), 256), i * 1568:(i + 1) * 1568] = v.reshape(1568, 256).T
            return carry

        lax.fori_loop(0, 3, tap, 0)

    def prepare_rpn():
        lane = lax.broadcasted_iota(jnp.int32, (256, 256), 1) % 32
        first = lane == 0
        last = lane == 31
        zero = jnp.zeros((256, 256), bf16)

        def piece(k, carry):
            col = pl.multiple_of(k * 256, 256)
            v = xr[pl.ds(col, 256), :].T
            xt[256:512, pl.ds(col, 256)] = v
            xt[0:256, pl.ds(col, 256)] = jnp.where(first, zero, pltpu.roll(v, 1, 1))
            xt[512:768, pl.ds(col, 256)] = jnp.where(last, zero, pltpu.roll(v, 255, 1))
            return carry

        lax.fori_loop(0, 12, piece, 0, unroll=4)

    def multiply(kind, a):
        if kind == 0:
            y = jnp.concatenate([ym[i, pl.ds(2 - a, 14)].reshape(1568, 256) for i in range(2)], 0)
            r = jnp.dot(xt[:, 0:3136], y, preferred_element_type=f32)
        else:
            y = jnp.concatenate([yr[1600 * i + 32 * (2 - a):1600 * i + 32 * (2 - a) + 1536, :] for i in range(2)], 0)
            r = jnp.dot(xt[:, 0:3072], y, preferred_element_type=f32)
        for h in range(2):
            grad[kind, a, h] = r[:, 128 * h:128 * h + 128].reshape(96, 8, 128)
        send(grad.at[kind, a, 1 - core], other.at[kind, a], pair_send.at[kind, a], pair_recv.at[kind, a], partner)

    def landed(dst, sem):
        pltpu.make_async_copy(dst, dst, sem).wait()

    def halves(kind, a):
        return part.at[kind, a], inbox.at[kind, a], ring_send.at[kind, a], ring_recv.at[kind, a], pos[a]

    def combine(kind, a):
        landed(other.at[kind, a], pair_recv.at[kind, a])
        total = grad[kind, a, core] + other[kind, a]
        s, box, ss, rs, i = halves(kind, a)
        s[...] = total.reshape(4, 24, 8, 128)
        right, left = along(a, 1), along(a, -1)
        far, nxt, prv = (lax.rem(i + d, RING) for d in (2, 1, 3))
        send(s.at[far, pl.ds(0, 12)], box.at[0], ss.at[0], rs.at[0], right)
        send(s.at[far, pl.ds(12, 12)], box.at[1], ss.at[1], rs.at[1], left)
        send(s.at[nxt, pl.ds(12, 12)], box.at[2], ss.at[2], rs.at[2], right)
        send(s.at[prv, pl.ds(0, 12)], box.at[3], ss.at[3], rs.at[3], left)

    def pass_on(kind, a):
        s, box, ss, rs, i = halves(kind, a)
        nxt, prv = lax.rem(i + 1, RING), lax.rem(i + 3, RING)
        landed(box.at[0], rs.at[0])
        relay[kind, a, 0] = s[nxt, 0:12] + box[0]
        send(relay.at[kind, a, 0], box.at[4], ss.at[4], rs.at[4], along(a, 1))
        landed(box.at[1], rs.at[1])
        relay[kind, a, 1] = s[prv, 12:24] + box[1]
        send(relay.at[kind, a, 1], box.at[5], ss.at[5], rs.at[5], along(a, -1))

    def finish(kind, a):
        s, box, ss, rs, i = halves(kind, a)
        for k in (2, 3, 4, 5):
            landed(box.at[k], rs.at[k])
        chunk[a, kind * 24:kind * 24 + 12] = s[i, 0:12] + box[3] + box[4]
        chunk[a, kind * 24 + 12:kind * 24 + 24] = s[i, 12:24] + box[2] + box[5]

    def plane(a, db, dc):
        offset = [0, 0, 0]
        offset[(a + 1) % 3] = db
        offset[(a + 2) % 3] = dc
        return at(offset)

    def place(a, db=0, dc=0):
        b, c = pos[(a + 1) % 3], pos[(a + 2) % 3]
        return lax.rem(b + db, RING) * 4 + lax.rem(c + dc, RING)

    def scatter(a):
        for k, (db, dc) in enumerate(PLANE):
            send(
                chunk.at[a, pl.ds(3 * place(a, db, dc), 3)], plane_in.at[a, k],
                plane_send.at[a, k], plane_recv.at[a, k], plane(a, db, dc),
            )

    def reduce_and_fan(a):
        p = place(a)
        total = chunk[a, pl.ds(3 * p, 3)]
        for k in range(15):
            landed(plane_in.at[a, k], plane_recv.at[a, k])
            total = total + plane_in[a, k]
        mine = full.at[core, a, pos[a], pl.ds(3 * p, 3)]
        mine[...] = total / count[4, p // 8][None]
        for k, (db, dc) in enumerate(PLANE):
            send(mine, mine, fan_send.at[a, k], fan_recv.at[a, k], plane(a, db, dc))

    def to_partner(a, j, lo, n, slot):
        piece = full.at[core, a, j, pl.ds(lo, n)]
        send(piece, piece, last_send.at[a, slot], last_recv.at[a, slot], partner)

    def gather_start(a):
        i = pos[a]
        for k, (db, dc) in enumerate(PLANE):
            p = place(a, RING - db if db else 0, RING - dc if dc else 0)
            landed(full.at[core, a, i, pl.ds(3 * p, 3)], fan_recv.at[a, k])
        right, left = along(a, 1), along(a, -1)
        lo, hi = (full.at[core, a, i, pl.ds(h, 24)] for h in (0, 24))
        send(lo, lo, ag_send.at[a, 0], ag_recv.at[a, 0], right)
        send(hi, hi, ag_send.at[a, 1], ag_recv.at[a, 1], left)
        send(hi, hi, ag_send.at[a, 2], ag_recv.at[a, 2], right)
        send(lo, lo, ag_send.at[a, 3], ag_recv.at[a, 3], left)
        to_partner(a, i, 0, 48, 0)

    def gather_pass(a):
        i = pos[a]
        nxt, prv = lax.rem(i + 1, RING), lax.rem(i + 3, RING)
        piece = full.at[core, a, prv, pl.ds(0, 24)]
        landed(piece, ag_recv.at[a, 0])
        send(piece, piece, ag_send.at[a, 4], ag_recv.at[a, 4], along(a, 1))
        to_partner(a, prv, 0, 24, 1)
        piece = full.at[core, a, nxt, pl.ds(24, 24)]
        landed(piece, ag_recv.at[a, 1])
        send(piece, piece, ag_send.at[a, 5], ag_recv.at[a, 5], along(a, -1))
        to_partner(a, nxt, 24, 24, 2)

    def gather_near(a):
        i = pos[a]
        nxt, prv = lax.rem(i + 1, RING), lax.rem(i + 3, RING)
        landed(full.at[core, a, prv, pl.ds(24, 24)], ag_recv.at[a, 2])
        to_partner(a, prv, 24, 24, 3)
        landed(full.at[core, a, nxt, pl.ds(0, 24)], ag_recv.at[a, 3])
        to_partner(a, nxt, 0, 24, 4)

    def gather_far(a):
        far = lax.rem(pos[a] + 2, RING)
        landed(full.at[core, a, far, pl.ds(0, 24)], ag_recv.at[a, 4])
        to_partner(a, far, 0, 24, 5)
        landed(full.at[core, a, far, pl.ds(24, 24)], ag_recv.at[a, 5])
        to_partner(a, far, 24, 24, 6)

    def from_partner(a, slot):
        i = pos[a]
        d, lo, n = ((0, 0, 48), (3, 0, 24), (1, 24, 24), (3, 24, 24), (1, 0, 24), (2, 0, 24), (2, 24, 24))[slot]
        landed(full.at[1 - core, a, lax.rem(i + d, RING), pl.ds(lo, n)], last_recv.at[a, slot])

    outs = ((out_wm, out_mm), (out_wr, out_mr))

    def update(a, d, kind, h):
        j = lax.rem(pos[a] + d, RING)
        g = full[h, a, j, kind * 24:kind * 24 + 24].reshape(192, 128)
        rows = pl.ds(pl.multiple_of(a * 768 + j * 192, 64), 192)
        lanes = pl.ds(pl.multiple_of(h * 128, 128), 128)
        new_w, new_m = outs[kind]
        m = 0.9 * moments[kind, rows, lanes] + g
        new_m[rows, lanes] = m
        new_w[rows, lanes] = weights[kind, rows, lanes] - 0.02 * m

    def count_pair():
        send(count.at[0], count_in.at[0], count_send.at[0], count_recv.at[0], partner)

    def count_axis(axis):
        if axis == 0:
            landed(count_in.at[0], count_recv.at[0])
            count[1] = count[0] + count_in[0]
        else:
            count_close(axis - 1)
        for d in (1, 2, 3):
            k = 3 * axis + d
            send(count.at[axis + 1], count_in.at[k], count_send.at[k], count_recv.at[k], along(axis, d))

    def count_close(axis):
        total = count[axis + 1]
        for d in (1, 2, 3):
            k = 3 * axis + d
            landed(count_in.at[k], count_recv.at[k])
            total = total + count_in[k]
        count[axis + 2] = total

    loads[0].wait()
    loads[1].wait()
    prepare_mask()
    pl.semaphore_wait(barrier, 1 + len(CUBE))
    count_pair()
    multiply(0, 0)
    count_axis(0)
    multiply(0, 1)
    combine(0, 0)
    count_axis(1)
    multiply(0, 2)
    pass_on(0, 0)
    combine(0, 1)
    count_axis(2)
    for copy in loads[2:5]:
        copy.wait()
    for copy in loads[5:]:
        copy.start()
    prepare_rpn()
    pass_on(0, 1)
    combine(0, 2)
    multiply(1, 0)
    pass_on(0, 2)
    finish(0, 0)
    multiply(1, 1)
    combine(1, 0)
    finish(0, 1)
    multiply(1, 2)
    pass_on(1, 0)
    combine(1, 1)
    finish(0, 2)
    count_close(2)
    combine(1, 2)
    pass_on(1, 1)
    finish(1, 0)
    scatter(0)
    pass_on(1, 2)
    finish(1, 1)
    scatter(1)
    finish(1, 2)
    scatter(2)
    for a in range(3):
        reduce_and_fan(a)
    for a in range(3):
        gather_start(a)
    for copy in loads[5:]:
        copy.wait()
    for a in range(3):
        gather_pass(a)
    for a in range(3):
        for kind in range(2):
            update(a, 0, kind, core)
    for a in range(3):
        gather_near(a)
    for a in range(3):
        for kind in range(2):
            update(a, 1, kind, core)
            update(a, 3, kind, core)
    for a in range(3):
        for slot in range(5):
            from_partner(a, slot)
        for kind in range(2):
            for d in (0, 1, 3):
                update(a, d, kind, 1 - core)
    for a in range(3):
        gather_far(a)
    for a in range(3):
        for kind in range(2):
            update(a, 2, kind, core)
    for a in range(3):
        for slot in (5, 6):
            from_partner(a, slot)
        for kind in range(2):
            update(a, 2, kind, 1 - core)
    for copy in sent:
        copy.wait_send()


def on_device(xm, ym, roi, xr, yr, anchor, wm, wr, mm, mr):
    images, slots, side, _, chans = xm.shape
    vmem = pltpu.VMEM
    dma = pltpu.SemaphoreType.DMA
    anywhere = pl.BlockSpec(memory_space=pl.ANY)
    smem = pl.BlockSpec(memory_space=pltpu.SMEM)
    shape = jax.ShapeDtypeStruct(wm.shape, f32)
    xm = xm.transpose(0, 2, 3, 1, 4)
    ym = ym.transpose(0, 2, 3, 1, 4)
    return pl.pallas_call(
        kernel,
        out_shape=(shape,) * 4,
        in_specs=[anywhere, anywhere, smem, anywhere, anywhere, smem] + [anywhere] * 4,
        out_specs=(pl.BlockSpec(memory_space=vmem),) * 4,
        scratch_shapes=[
            vmem((2, 14, 16, 8, 256), bf16),
            vmem((2, 16, 14, 8, 256), bf16),
            vmem((3072, 256), bf16),
            vmem((3200, 256), bf16),
            vmem((768, 3200), bf16),
            vmem((2, 3, 2, 96, 8, 128), f32),
            vmem((2, 3, 96, 8, 128), f32),
            vmem((2, 3, 4, 24, 8, 128), f32),
            vmem((2, 3, 6, 12, 8, 128), f32),
            vmem((2, 3, 2, 12, 8, 128), f32),
            vmem((3, 48, 8, 128), f32),
            vmem((3, 15, 3, 8, 128), f32),
            vmem((2, 3, 4, 48, 8, 128), f32),
            vmem((2, 2304, 256), f32),
            vmem((2, 2304, 256), f32),
            vmem((5, 2, 8, 128), f32),
            vmem((10, 2, 8, 128), f32),
            dma((9,)),
            dma((2, 3)), dma((2, 3)),
            dma((2, 3, 6)), dma((2, 3, 6)),
            dma((3, 15)), dma((3, 15)),
            dma((3, 15)), dma((3, 15)),
            dma((3, 6)), dma((3, 6)),
            dma((3, 7)), dma((3, 7)),
            dma((10,)), dma((10,)),
        ],
        compiler_params=pltpu.CompilerParams(
            collective_id=0, has_side_effects=True, vmem_limit_bytes=62 << 20
        ),
    )(xm, ym, roi, xr.reshape(-1, chans), yr.reshape(-1, chans), anchor, wm, wr, mm, mr)


def solution(mesh):
    images = ("gx", "gy")
    placed = (
        P(images, None, None, None, None),
        P(images, None, None, None, None),
        P(images),
        P(images, None, None, None),
        P(images, None, None, None),
        P(images),
        P(), P(), P(), P(),
    )
    return jax.shard_map(
        on_device, mesh=mesh, in_specs=placed, out_specs=(P(), P(), P(), P()), check_vma=False
    )
```

time: 271 us -> 84.6 us (0.31)
  waiting for transfers between devices: 85.5 us -> 0 us
  Pallas kernels: 0 us -> 73.9 us
  blocking collectives: 69.6 us -> 0 us
  local copies, waits for them, and re-layouts: 54.6 us -> 9.81 us
  matrix products: 30 us -> 0 us
  other arithmetic: 15.6 us -> 0 us
  between operations: 14.2 us -> 0.65 us
    psum x1 -> x0, waiting for transfers between devices: 85.5 us -> none  [on_device(): lax.psum((mask_local, rpn_local, local_counts), ('gx', 'gy'))]
    pallas_call x0 -> x1, Pallas kernels: none -> 73.9 us  [on_device(): pl.pallas_call(kernel, out_shape=(shape,) * 4, in_specs=[anywhere, anywhe...]
    psum x1 -> x0, blocking collectives: 69.6 us -> none  [on_device(): lax.psum((mask_local, rpn_local, local_counts), ('gx', 'gy'))]
    dot_general x18 -> x0, matrix products: 30 us -> none  [weight_grad(): lax.dot_general(window, flat_cot, (((0,), (0,)), ((), ())), preferred_ele...]
    slice x10 -> x0, local copies, waits for them, and re-layouts: 23.3 us -> none  [the longest x9 22.6 us: weight_grad(): padded[:, row_tap:row_tap + grid_rows, col_tap:col_tap + grid_cols, :]]
    reshape x8 -> x0, local copies, waits for them, and re-layouts: 20.2 us -> none  [weight_grad(): window = padded[:, row_tap:row_tap + grid_rows, col_tap:col_tap + grid_co...]
    sub x1 -> x0, other arithmetic: 10.6 us -> none  [step_update(): return (weight - 0.02 * fresh_moment, fresh_moment)]
    unnamed x34 -> x10, local copies, waits for them, and re-layouts: 5.92 us -> 9.81 us
  transfers between devices with their start and end apart: 1 -> 0, of which waited for: 1 -> 0; matrix products, arithmetic and copies ran while one was open for 1% -> 0% of each run, Pallas kernels for 0% -> 0%
where the time goes in v1:
time: 84.6 us; the launch traced here: 84.4 us
  Pallas kernels  73.9 us (87%)
  local copies, waits for them, and re-layouts  9.81 us (12%)
    pallas_call x1, Pallas kernels, on_device(): pl.pallas_call(kernel, out_shape=(shape,) * 4, in_specs=[anywhere, anywhe...  73.9 us
    unnamed x10, local copies, waits for them, and re-layouts  9.81 us

profile of v1, /device:TPU:1, one launch (start us, length us, event | category | flops | bytes accessed | tf_op | source)
XLA Modules:
  0.0 84.4 jit_solution(16518672738364784072)
XLA Ops:
  0.6 73.9 %shard_map.129 = (f32[2304,256]{1,0:T(8,128)}, f32[2304,256]{1,0:T(8,128)}, f32[2304,256]{1,0:T(8,128)}, f32[2304,256]{1,0:T(8,128)}) custom-call(bf16[2,14,14,8,256]{4,3,2,1,0:T(8,128)(2,1)} %bitcast.4, bf16[2,14,14,8,256]{4,3,2,1,0:T(8,128)(2,1)} %bitcast.5, s32[2]{0:T(128)} %roi.1, bf16[3072,256]{1,0:T(8,128)(2,1)} %bitcast.6, bf16[3072,256]{1,0:T(8,128)(2,1)} %bitcast.7, ...), custom_call_target="tpu_custom_call" | custom-call | tf_op jit(solution)/shard_map/pallas_call | solution.py:357
  74.6 0.0 copy-start.2
  74.6 3.4 %copy.18 = f32[2304,256]{1,0:T(8,128)} copy(f32[2304,256]{1,0:T(8,128)} %get-tuple-element.8) | data formatting | bytes 4718592
  77.9 0.0 copy-done.2
  77.9 0.0 copy-start.1
  77.9 1.4 %copy.19 = f32[2304,256]{1,0:T(8,128)} copy(f32[2304,256]{1,0:T(8,128)S(1)} %copy-done.2) | data formatting | bytes 4718592
  79.3 1.1 %copy-done.1 = f32[2304,256]{1,0:T(8,128)S(1)} copy-done((f32[2304,256]{1,0:T(8,128)S(1)}, f32[2304,256]{1,0:T(8,128)}, u32[]{:S(2)}) %copy-start.1) | copy-done | bytes 2359320
  80.5 0.0 copy-start
  80.5 1.4 %copy.20 = f32[2304,256]{1,0:T(8,128)} copy(f32[2304,256]{1,0:T(8,128)S(1)} %copy-done.1) | data formatting | bytes 4718592
  81.9 1.1 %copy-done = f32[2304,256]{1,0:T(8,128)S(1)} copy-done((f32[2304,256]{1,0:T(8,128)S(1)}, f32[2304,256]{1,0:T(8,128)}, u32[]{:S(2)}) %copy-start) | copy-done | bytes 2359320
  83.0 1.4 %copy.21 = f32[2304,256]{1,0:T(8,128)} copy(f32[2304,256]{1,0:T(8,128)S(1)} %copy-done) | data formatting | bytes 4718592
Async XLA Ops:
  74.6 3.4 %copy-start.2 = (f32[2304,256]{1,0:T(8,128)S(1)}, f32[2304,256]{1,0:T(8,128)}, u32[]{:S(2)}) copy-start(f32[2304,256]{1,0:T(8,128)} %get-tuple-element.9) | copy-start | bytes 7077892
  77.9 2.5 %copy-start.1 = (f32[2304,256]{1,0:T(8,128)S(1)}, f32[2304,256]{1,0:T(8,128)}, u32[]{:S(2)}) copy-start(f32[2304,256]{1,0:T(8,128)} %get-tuple-element.10) | copy-start | bytes 7077892
  80.5 2.5 %copy-start = (f32[2304,256]{1,0:T(8,128)S(1)}, f32[2304,256]{1,0:T(8,128)}, u32[]{:S(2)}) copy-start(f32[2304,256]{1,0:T(8,128)} %get-tuple-element.11) | copy-start | bytes 7077892

commit v2 on v1

v2 whole, which is shorter than its diff:
```python
import jax
import jax.numpy as jnp
from jax import lax
from jax.experimental import pallas as pl
from jax.experimental.pallas import tpu as pltpu
from jax.sharding import PartitionSpec as P

bf16 = jnp.bfloat16
f32 = jnp.float32
RING = 4
AWAY = (1, 3, 2)
PLANE = sorted(
    ((db, dc) for db in range(4) for dc in range(4) if (db, dc) != (0, 0)),
    key=lambda d: min(d[0], 4 - d[0]) + min(d[1], 4 - d[1]),
)
CUBE = [
    (dx, dy, dz)
    for dx in range(4)
    for dy in range(4)
    for dz in range(4)
    if 1 <= (dx != 0) + (dy != 0) + (dz != 0) <= 2
]
JOBS = tuple((kind, a) for kind in range(2) for a in range(3))


def kernel(
    xm_hbm, ym_hbm, roi, xr_hbm, yr_hbm, anchor, wm_hbm, wr_hbm, mm_hbm, mr_hbm,
    out_wm, out_wr, out_mm, out_mr,
    xm, ym, xr, yr, xt, grad, other, part, inbox, line, plane_in, full,
    weights, moments, count, count_in,
    load_sem, pair_send, pair_recv, one_send, one_recv, plane_send, plane_recv, fan_send, fan_recv,
    back1_send, back1_recv, last_send, last_recv,
    count_send, count_recv,
):
    gx = lax.axis_index("gx")
    gy = lax.axis_index("gy")
    core = lax.rem(gx, 2)
    pos = (gx // 2, lax.rem(gy, 4), gy // 4)

    def at(offset, own_core=True):
        x, y, z = (lax.rem(p + d, RING) if d else p for p, d in zip(pos, offset))
        return (x * 2 + (core if own_core else 1 - core), z * 4 + y)

    def along(axis, d):
        offset = [0, 0, 0]
        offset[axis] = d % RING
        return at(offset)

    def start(src, dst, send_sem, recv_sem, device):
        copy = pltpu.make_async_remote_copy(
            src_ref=src, dst_ref=dst, send_sem=send_sem, recv_sem=recv_sem,
            device_id=device, device_id_type=pl.DeviceIdType.MESH,
        )
        copy.start()
        return copy

    def send(*args):
        sent.append(start(*args))

    sent = []
    partner = at((0, 0, 0), own_core=False)

    loads = [
        pltpu.make_async_copy(xm_hbm, xm.at[:, :, pl.ds(1, 14)], load_sem.at[0]),
        pltpu.make_async_copy(ym_hbm, ym.at[:, pl.ds(1, 14)], load_sem.at[1]),
        pltpu.make_async_copy(xr_hbm, xr, load_sem.at[2]),
        pltpu.make_async_copy(yr_hbm.at[pl.ds(0, 1536)], yr.at[pl.ds(32, 1536)], load_sem.at[3]),
        pltpu.make_async_copy(yr_hbm.at[pl.ds(1536, 1536)], yr.at[pl.ds(1632, 1536)], load_sem.at[4]),
        pltpu.make_async_copy(mm_hbm, moments.at[0], load_sem.at[5]),
        pltpu.make_async_copy(mr_hbm, moments.at[1], load_sem.at[6]),
        pltpu.make_async_copy(wm_hbm, weights.at[0], load_sem.at[7]),
        pltpu.make_async_copy(wr_hbm, weights.at[1], load_sem.at[8]),
    ]
    for copy in loads[:2]:
        copy.start()
    barrier = pltpu.get_barrier_semaphore()
    for device in [partner] + [at(o) for o in CUBE]:
        pl.semaphore_signal(barrier, inc=1, device_id=device, device_id_type=pl.DeviceIdType.MESH)
    for i in range(2):
        for e in (0, 15):
            xm[i, :, e] = jnp.zeros((14, 8, 256), bf16)
            ym[i, e] = jnp.zeros((14, 8, 256), bf16)
        for e in (0, 49):
            yr[pl.ds(1600 * i + 32 * e, 32), :] = jnp.zeros((32, 256), bf16)

    count[0, 0] = jnp.full((8, 128), (roi[0] + roi[1]).astype(f32))
    count[0, 1] = jnp.full((8, 128), (anchor[0] + anchor[1]).astype(f32))

    def prepare_mask():
        slot = lax.broadcasted_iota(jnp.int32, (8, 256), 0)

        def tap(b, carry):
            for i in range(2):
                keep = slot < roi[i]
                v = xm[i, :, pl.ds(b, 14)]
                v = jnp.where(keep[None, None], v, jnp.zeros_like(v))
                xt[pl.ds(pl.multiple_of(b * 256, 256), 256), i * 1568:(i + 1) * 1568] = v.reshape(1568, 256).T
            return carry

        lax.fori_loop(0, 3, tap, 0)

    def prepare_rpn():
        lane = lax.broadcasted_iota(jnp.int32, (256, 256), 1) % 32
        first = lane == 0
        last = lane == 31
        zero = jnp.zeros((256, 256), bf16)

        def piece(k, carry):
            col = pl.multiple_of(k * 256, 256)
            v = xr[pl.ds(col, 256), :].T
            xt[256:512, pl.ds(col, 256)] = v
            xt[0:256, pl.ds(col, 256)] = jnp.where(first, zero, pltpu.roll(v, 1, 1))
            xt[512:768, pl.ds(col, 256)] = jnp.where(last, zero, pltpu.roll(v, 255, 1))
            return carry

        lax.fori_loop(0, 12, piece, 0, unroll=4)

    def multiply(kind, a):
        if kind == 0:
            y = jnp.concatenate([ym[i, pl.ds(2 - a, 14)].reshape(1568, 256) for i in range(2)], 0)
        else:
            y = jnp.concatenate([yr[1600 * i + 32 * (2 - a):1600 * i + 32 * (2 - a) + 1536, :] for i in range(2)], 0)
        for m in range(2):
            r = jnp.dot(xt[384 * m:384 * m + 384, 0:y.shape[0]], y, preferred_element_type=f32)
            for h in range(2):
                grad[kind, a, h, 48 * m:48 * m + 48] = r[:, 128 * h:128 * h + 128].reshape(48, 8, 128)

    def exchange(kind, a):
        send(grad.at[kind, a, 1 - core], other.at[kind, a], pair_send.at[kind, a], pair_recv.at[kind, a], partner)

    def landed(dst, sem):
        pltpu.make_async_copy(dst, dst, sem).wait()

    def combine(job):
        kind, a = JOBS[job]
        landed(other.at[kind, a], pair_recv.at[kind, a])
        total = grad[kind, a, core] + other[kind, a]
        part[job] = total.reshape(3, RING, 8, 8, 128)
        for c in range(3):
            for slot, d in enumerate(AWAY):
                send(
                    part.at[job, c, lax.rem(pos[c] + d, RING)], inbox.at[job, c, slot],
                    one_send.at[job, c, slot], one_recv.at[job, c, slot], along(c, d),
                )

    def first(job):
        for c in range(3):
            total = part[job, c, pos[c]]
            for slot in range(3):
                landed(inbox.at[job, c, slot], one_recv.at[job, c, slot])
                total = total + inbox[job, c, slot]
            line[c, 8 * job:8 * job + 8] = total

    def plane(c, db, dc):
        offset = [0, 0, 0]
        offset[(c + 1) % 3] = db
        offset[(c + 2) % 3] = dc
        return at(offset)

    def place(c, db=0, dc=0):
        b, k = pos[(c + 1) % 3], pos[(c + 2) % 3]
        return pl.ds(12 * lax.rem(b + db, RING) + 3 * lax.rem(k + dc, RING), 3)

    def scatter(c):
        for k, (db, dc) in enumerate(PLANE):
            send(
                line.at[c, place(c, db, dc)], plane_in.at[c, k],
                plane_send.at[c, k], plane_recv.at[c, k], plane(c, db, dc),
            )

    def fan(c):
        total = line[c, place(c)]
        for k in range(15):
            landed(plane_in.at[c, k], plane_recv.at[c, k])
            total = total + plane_in[c, k]
        mine = full.at[core, c, pos[c], place(c)]
        mine[...] = total / count[4, pos[(c + 1) % 3] // 2][None]
        for k, (db, dc) in enumerate(PLANE):
            send(mine, mine, fan_send.at[c, k], fan_recv.at[c, k], plane(c, db, dc))

    def gathered(c, d, h):
        return full.at[h, c, lax.rem(pos[c] + d, RING)]

    def half(c, d, h):
        return full.at[core, c, lax.rem(pos[c] + d, RING), pl.ds(24 * h, 24)]

    def share(c, d, h, slot, step):
        piece = half(c, d, h)
        send(piece, piece, back1_send.at[c, slot], back1_recv.at[c, slot], along(c, step))

    def to_partner(c, d):
        piece = gathered(c, d, core)
        send(piece, piece, last_send.at[c, d], last_recv.at[c, d], partner)

    def back1(c):
        for k, (db, dc) in enumerate(PLANE):
            landed(full.at[core, c, pos[c], place(c, (4 - db) % 4, (4 - dc) % 4)], fan_recv.at[c, k])
        share(c, 0, 0, 0, 1)
        share(c, 0, 1, 1, 3)
        share(c, 0, 1, 2, 1)
        share(c, 0, 0, 3, 3)
        to_partner(c, 0)

    def relay(c):
        landed(half(c, 3, 0), back1_recv.at[c, 0])
        share(c, 3, 0, 4, 1)
        landed(half(c, 1, 1), back1_recv.at[c, 1])
        share(c, 1, 1, 5, 3)

    def near(c):
        landed(half(c, 3, 1), back1_recv.at[c, 2])
        to_partner(c, 3)
        landed(half(c, 1, 0), back1_recv.at[c, 3])
        to_partner(c, 1)

    def far(c):
        landed(half(c, 2, 0), back1_recv.at[c, 4])
        landed(half(c, 2, 1), back1_recv.at[c, 5])
        to_partner(c, 2)

    outs = ((out_wm, out_mm), (out_wr, out_mr))

    def update(c, d, h):
        j = lax.rem(pos[c] + d, RING)
        lanes = pl.ds(pl.multiple_of(h * 128, 128), 128)
        for job, (kind, a) in enumerate(JOBS):
            g = full[h, c, j, 8 * job:8 * job + 8].reshape(64, 128)
            rows = pl.ds(pl.multiple_of(a * 768 + c * 256 + j * 64, 64), 64)
            new_w, new_m = outs[kind]
            m = 0.9 * moments[kind, rows, lanes] + g
            new_m[rows, lanes] = m
            new_w[rows, lanes] = weights[kind, rows, lanes] - 0.02 * m

    def own(c, d):
        update(c, d, core)

    def theirs(c, d):
        landed(gathered(c, d, 1 - core), last_recv.at[c, d])
        update(c, d, 1 - core)

    def count_pair():
        send(count.at[0], count_in.at[0], count_send.at[0], count_recv.at[0], partner)

    def count_axis(axis):
        if axis == 0:
            landed(count_in.at[0], count_recv.at[0])
            count[1] = count[0] + count_in[0]
        else:
            count_close(axis - 1)
        for d in (1, 2, 3):
            k = 3 * axis + d
            send(count.at[axis + 1], count_in.at[k], count_send.at[k], count_recv.at[k], along(axis, d))

    def count_close(axis):
        total = count[axis + 1]
        for d in (1, 2, 3):
            k = 3 * axis + d
            landed(count_in.at[k], count_recv.at[k])
            total = total + count_in[k]
        count[axis + 2] = total

    def later_loads():
        for copy in loads[2:5]:
            copy.wait()
        for copy in loads[5:]:
            copy.start()

    def weights_in():
        for copy in loads[5:]:
            copy.wait()

    def enter():
        pl.semaphore_wait(barrier, 1 + len(CUBE))

    steps = [
        (multiply, 0, 0,),
        (enter,),
        (exchange, 0, 0,),
        (count_pair,),
        (multiply, 0, 1,),
        (exchange, 0, 1,),
        (count_axis, 0,),
        (combine, 0,),
        (multiply, 0, 2,),
        (exchange, 0, 2,),
        (combine, 1,),
        (later_loads,),
        (prepare_rpn,),
        (count_axis, 1,),
        (combine, 2,),
        (multiply, 1, 0,),
        (exchange, 1, 0,),
        (multiply, 1, 1,),
        (exchange, 1, 1,),
        (first, 0,),
        (combine, 3,),
        (multiply, 1, 2,),
        (exchange, 1, 2,),
        (combine, 4,),
        (count_axis, 2,),
        (first, 1,),
        (first, 2,),
        (combine, 5,),
        (first, 3,),
        (count_close, 2,),
        (first, 4,),
        (first, 5,),
        (scatter, 0,),
        (scatter, 1,),
        (scatter, 2,),
        (fan, 0,),
        (fan, 1,),
        (fan, 2,),
        (back1, 0,),
        (back1, 1,),
        (back1, 2,),
        (weights_in,),
        (own, 0, 0,),
        (own, 1, 0,),
        (own, 2, 0,),
        (relay, 0,),
        (relay, 1,),
        (relay, 2,),
        (theirs, 0, 0,),
        (theirs, 1, 0,),
        (theirs, 2, 0,),
        (near, 0,),
        (near, 1,),
        (near, 2,),
        (own, 0, 3,),
        (own, 0, 1,),
        (own, 1, 3,),
        (own, 1, 1,),
        (own, 2, 3,),
        (own, 2, 1,),
        (theirs, 0, 3,),
        (theirs, 0, 1,),
        (theirs, 1, 3,),
        (theirs, 1, 1,),
        (theirs, 2, 3,),
        (theirs, 2, 1,),
        (far, 0,),
        (far, 1,),
        (far, 2,),
        (own, 0, 2,),
        (own, 1, 2,),
        (own, 2, 2,),
        (theirs, 0, 2,),
        (theirs, 1, 2,),
        (theirs, 2, 2,),
    ]
    loads[0].wait()
    loads[1].wait()
    for copy in loads[2:5]:
        copy.start()
    prepare_mask()
    for step, *args in steps:
        step(*args)
    for copy in sent:
        copy.wait_send()


def write_out(*refs):
    sem = refs[8]
    rows = refs[0].shape[0] // 2
    copies = [
        pltpu.make_async_copy(refs[k].at[pl.ds(h * rows, rows)], refs[4 + k].at[pl.ds(h * rows, rows)], sem.at[2 * k + h])
        for k in range(4) for h in range(2)
    ]
    for copy in copies:
        copy.start()
    for copy in copies:
        copy.wait()


def on_device(xm, ym, roi, xr, yr, anchor, wm, wr, mm, mr):
    images, slots, side, _, chans = xm.shape
    vmem = pltpu.VMEM
    dma = pltpu.SemaphoreType.DMA
    anywhere = pl.BlockSpec(memory_space=pl.ANY)
    smem = pl.BlockSpec(memory_space=pltpu.SMEM)
    shape = jax.ShapeDtypeStruct(wm.shape, f32)
    xm = xm.transpose(0, 2, 3, 1, 4)
    ym = ym.transpose(0, 2, 3, 1, 4)
    results = pl.pallas_call(
        kernel,
        out_shape=(vmem(wm.shape, f32),) * 4,
        in_specs=[anywhere, anywhere, smem, anywhere, anywhere, smem] + [anywhere] * 4,
        out_specs=(pl.BlockSpec(memory_space=vmem),) * 4,
        scratch_shapes=[
            vmem((2, 14, 16, 8, 256), bf16),
            vmem((2, 16, 14, 8, 256), bf16),
            vmem((3072, 256), bf16),
            vmem((3200, 256), bf16),
            vmem((768, 3200), bf16),
            vmem((2, 3, 2, 96, 8, 128), f32),
            vmem((2, 3, 96, 8, 128), f32),
            vmem((6, 3, RING, 8, 8, 128), f32),
            vmem((6, 3, 3, 8, 8, 128), f32),
            vmem((3, 48, 8, 128), f32),
            vmem((3, 15, 3, 8, 128), f32),
            vmem((2, 3, RING, 48, 8, 128), f32),
            vmem((2, 2304, 256), f32),
            vmem((2, 2304, 256), f32),
            vmem((5, 2, 8, 128), f32),
            vmem((10, 2, 8, 128), f32),
            dma((9,)),
            dma((2, 3)), dma((2, 3)),
            dma((6, 3, 3)), dma((6, 3, 3)),
            dma((3, 15)), dma((3, 15)),
            dma((3, 15)), dma((3, 15)),
            dma((3, 6)), dma((3, 6)),
            dma((3, RING)), dma((3, RING)),
            dma((10,)), dma((10,)),
        ],
        compiler_params=pltpu.CompilerParams(
            collective_id=0, has_side_effects=True, vmem_limit_bytes=57606144
        ),
    )(xm, ym, roi, xr.reshape(-1, chans), yr.reshape(-1, chans), anchor, wm, wr, mm, mr)
    return pl.pallas_call(
        write_out,
        out_shape=(shape,) * 4,
        in_specs=[pl.BlockSpec(memory_space=vmem)] * 4,
        out_specs=(anywhere,) * 4,
        scratch_shapes=[dma((8,))],
        compiler_params=pltpu.CompilerParams(vmem_limit_bytes=1 << 20),
    )(*results)


def solution(mesh):
    images = ("gx", "gy")
    placed = (
        P(images, None, None, None, None),
        P(images, None, None, None, None),
        P(images),
        P(images, None, None, None),
        P(images, None, None, None),
        P(images),
        P(), P(), P(), P(),
    )
    return jax.shard_map(
        on_device, mesh=mesh, in_specs=placed, out_specs=(P(), P(), P(), P()), check_vma=False
    )
```

time: 84.6 us -> 60.5 us (0.72)
  Pallas kernels: 73.9 us -> 59.7 us
  local copies, waits for them, and re-layouts: 9.81 us -> 0 us
    pallas_call x1 -> x2, Pallas kernels: 73.9 us -> 59.7 us  [the longest x1 56 us: on_device(): pl.pallas_call(kernel, out_shape=(vmem(wm.shape, f32),) * 4, in_specs=[an...]
    unnamed x10 -> x0, local copies, waits for them, and re-layouts: 9.81 us -> none
where the time goes in v2:
time: 60.5 us; the launch traced here: 60.4 us
  Pallas kernels  59.7 us (99%)
  between operations  0.64 us (1%)
    pallas_call x1, Pallas kernels, on_device(): pl.pallas_call(kernel, out_shape=(vmem(wm.shape, f32),) * 4, in_specs=[an...  56 us
    pallas_call x1, Pallas kernels, on_device(): pl.pallas_call(write_out, out_shape=(shape,) * 4, in_specs=[pl.BlockSpec(...  3.7 us

profile of v2, /device:TPU:1, one launch (start us, length us, event | category | flops | bytes accessed | tf_op | source)
XLA Modules:
  0.0 60.4 jit_solution(18056567353886153567)
XLA Ops:
  0.6 56.0 %shard_map.129 = (f32[2304,256]{1,0:T(8,128)S(1)}, f32[2304,256]{1,0:T(8,128)S(1)}, f32[2304,256]{1,0:T(8,128)S(1)}, f32[2304,256]{1,0:T(8,128)S(1)}) custom-call(bf16[2,14,14,8,256]{4,3,2,1,0:T(8,128)(2,1)} %bitcast.4, bf16[2,14,14,8,256]{4,3,2,1,0:T(8,128)(2,1)} %bitcast.5, s32[2]{0:T(128)} %roi.1, bf16[3072,256]{1,0:T(8,128)(2,1)} %bitcast.6, ...), custom_call_target="tpu_custom_call" | custom-call | tf_op jit(solution)/shard_map/pallas_call | solution.py:385
  56.6 3.7 %shard_map.130 = (f32[2304,256]{1,0:T(8,128)}, f32[2304,256]{1,0:T(8,128)}, f32[2304,256]{1,0:T(8,128)}, f32[2304,256]{1,0:T(8,128)}) custom-call(f32[2304,256]{1,0:T(8,128)S(1)} %get-tuple-element.8.refs_0_, f32[2304,256]{1,0:T(8,128)S(1)} %get-tuple-element.9.refs_1_, f32[2304,256]{1,0:T(8,128)S(1)} %get-tuple-element.10.refs_2_, ...), custom_call_target="tpu_custom_call" | custom-call | tf_op jit(solution)/shard_map/pallas_call | solution.py:420
